TPU v7x, 32 devices: a whole 2x2x4 slice. The times are simulated.
32 devices in a mesh: user: 16 (over z, y, x), seq: 2 (over core).
Axes of the slice: x: 2, y: 2, z: 4, core: 2. Of those that a mesh axis runs over, the one named last changes fastest.
Arguments:
- behaviors: bfloat16 [32, 2048, 256], P('user', 'seq'), may hold values from -20 to 20
- candidates: bfloat16 [32, 64, 256], P('user', 'seq'), may hold values from -64 to 64
- ranks: int32 [32, 2, 128], P('user', 'seq'), may hold values from 0 to 1151, as said below
- lengths: int32 [32], P('user'), may hold values from 1024 to 2048
- hash_planes: bfloat16 [256, 64], replicated, may hold values from -0.375 to 0.375
- norm_gain: float32 [256], replicated, may hold values from 0.5 to 1.5
- norm_bias: float32 [256], replicated, may hold values from -3 to 3
Outputs:
- interest: bfloat16 [32, 64, 256], P('user', 'seq')
Inputs may be any that keep to these rules, and one draw needn't show every extreme that they name: ranks[u, s, :] are 128 distinct positions of group s's window of 1152 behaviors; on the first group all are 128 or more.
All inputs are finite; a program needn't handle non-finite values.
Results may differ from a plain program's by a relative error of at most 0.0023.
Values may be sent and summed in bfloat16 or wider, within the bound.
No kernel may reach another device: no remote copies, remote signals or barrier semaphores. Data moves between devices by JAX's collectives and lax.ppermute only.
A program may use at most 64 MiB of HBM per device.

v0:
```python
import math
import jax
import jax.numpy as jnp
from jax import lax
from jax.sharding import PartitionSpec as P

HALO = 128
NEG_FILL = -1e30
HASH_WEIGHT = 2.0
NORM_EPS = 1e-05


def passed_along(value, axis, steps):
    count = lax.axis_size(axis)
    first, last = (max(0, -steps), min(count, count - steps))
    return lax.ppermute(value, axis, [(source, source + steps) for source in range(first, last)])


def joined(shard, axis, combine):
    everything = jax.tree.map(lambda part: lax.all_gather(part, axis), shard)
    first = jax.tree.map(lambda part: part[0], everything)

    def turn(k, so_far):
        return combine(so_far, jax.tree.map(lambda part: part[k], everything))

    return lax.fori_loop(1, lax.axis_size(axis), turn, first)


def soft_codes(rows, hash_planes):
    return jnp.tanh(jnp.dot(rows, hash_planes, preferred_element_type=jnp.float32)).astype(
        jnp.bfloat16
    )


def combine_parts(left_part, right_part):
    joint_max = jnp.maximum(left_part[0], right_part[0])
    left_scale = jnp.exp(left_part[0] - joint_max)
    right_scale = jnp.exp(right_part[0] - joint_max)
    total_sum = left_part[1] * left_scale + right_part[1] * right_scale
    vector_sum = left_part[2] * left_scale[..., None] + right_part[2] * right_scale[..., None]
    return (joint_max, total_sum, vector_sum)


def shards(behaviors, candidates, ranks, lengths, hash_planes, norm_gain, norm_bias):
    group_rows = behaviors.shape[1]
    feature_width = behaviors.shape[2]
    own_cands = candidates.shape[1]
    code_bits = hash_planes.shape[1]
    seq_index = lax.axis_index("seq")
    tail_rows = behaviors[:, group_rows - HALO :, :]
    before = passed_along(tail_rows, "seq", 1)
    queries = lax.all_gather(candidates, "seq", axis=1, tiled=True)
    window_pos = ranks[:, 0, :]
    from_tail = window_pos < HALO
    tail_index = jnp.clip(window_pos, 0, HALO - 1)
    own_index = jnp.clip(window_pos - HALO, 0, group_rows - 1)
    take_rows = jax.vmap(lambda row_table, where_at: row_table[where_at])
    picked = jnp.where(
        from_tail[:, :, None], take_rows(before, tail_index), take_rows(behaviors, own_index)
    )
    position = seq_index * group_rows - HALO + window_pos
    usable = (position >= 0) & (position < lengths[:, None])
    query_codes = soft_codes(queries, hash_planes)
    picked_codes = soft_codes(picked, hash_planes)
    similar = jnp.einsum("ucd,ukd->uck", queries, picked, preferred_element_type=jnp.float32)
    agreement = jnp.einsum(
        "ucb,ukb->uck", query_codes, picked_codes, preferred_element_type=jnp.float32
    )
    scores = similar * (1.0 / math.sqrt(feature_width)) + HASH_WEIGHT / code_bits * agreement
    usable_rows = usable[:, None, :]
    group_max = jnp.max(jnp.where(usable_rows, scores, NEG_FILL), axis=2)
    weights = jnp.where(usable_rows, jnp.exp(scores - group_max[..., None]), 0.0)
    group_total = jnp.sum(weights, axis=2)
    group_sum = jnp.einsum(
        "uck,ukd->ucd", weights.astype(jnp.bfloat16), picked, preferred_element_type=jnp.float32
    )
    merged = joined((group_max, group_total, group_sum), "seq", combine_parts)
    denominator = lax.dynamic_slice_in_dim(merged[1], seq_index * own_cands, own_cands, 1)
    numerator = lax.dynamic_slice_in_dim(merged[2], seq_index * own_cands, own_cands, 1)
    attended = numerator / denominator[..., None]
    moments = lax.psum(
        (jnp.sum(attended, axis=(0, 1)), jnp.sum(attended * attended, axis=(0, 1))), ("user", "seq")
    )
    row_count = attended.shape[0] * own_cands * lax.axis_size("user") * lax.axis_size("seq")
    feature_mean = moments[0] / row_count
    feature_var = moments[1] / row_count - feature_mean * feature_mean
    normed = (attended - feature_mean) * lax.rsqrt(feature_var + NORM_EPS) * norm_gain + norm_bias
    return normed.astype(jnp.bfloat16)


def solution(mesh):
    in_specs = (
        P("user", "seq", None),
        P("user", "seq", None),
        P("user", "seq", None),
        P("user"),
        P(),
        P(),
        P(),
    )
    out_specs = P("user", "seq", None)
    return jax.shard_map(shards, mesh=mesh, in_specs=in_specs, out_specs=out_specs, check_vma=False)
```

profile of v0, /device:TPU:0, one launch (start us, length us, event | category | flops | bytes accessed | tf_op | source)
XLA Modules:
  0.0 59.7 jit_solution(5533782162240582082)
XLA Ops:
  0.0 0.0 copy-start
  0.0 0.9 %slice.15 = bf16[2,128,256]{2,1,0:T(8,128)(2,1)S(1)} slice(bf16[2,1024,256]{2,1,0:T(8,128)(2,1)} %param.7), slice={[0:2], [896:1024], [0:256]} | slice | bytes 262144 | tf_op jit(solution)/shard_map/slice | solution.py:50
  1.0 0.0 copy-start.1
  1.0 2.4 %collective-permute-start = (bf16[2,128,256]{2,1,0:T(8,128)(2,1)S(1)}, bf16[2,128,256]{2,1,0:T(8,128)(2,1)S(1)}, u32[]{:S(2)}, u32[]{:S(2)}) collective-permute-start(bf16[2,128,256]{2,1,0:T(8,128)(2,1)S(1)} %slice.15), channel_id=1, source_target_pairs={{0,1},{2,3},{4,5},{6,7},{8,9},{10,11},{12,13},{14,15},{16,17},{18,... | collective-permute-start | bytes 393224 | tf_op jit(solution)/shard_map/ppermute | solution.py:16
  3.4 0.1 compare_and_fusion
  3.5 1.9 %all_gather.21 = bf16[2,64,256]{2,1,0:T(8,128)(2,1)S(1)} all-gather(bf16[2,32,256]{2,1,0:T(8,128)(2,1)S(1)} %copy-done.1), channel_id=1, replica_groups=mesh['user'=16,'seq'=2] {'seq'}, dimensions={1}, use_global_device_ids=true | all-gather | bytes 98304 | tf_op jit(solution)/shard_map/all_gather | solution.py:52
  5.4 2.8 %gather_fusion.1 = bf16[256,256]{1,0:T(8,128)(2,1)S(1)} fusion(bf16[2,1024,256]{2,1,0:T(8,128)(2,1)} %param.7, s32[256]{0:T(256)S(1)} %fusion.27), kind=kCustom, calls=%fused_computation.1 | custom fusion | bytes 264192 | tf_op jit(solution)/shard_map/vmap()/gather | solution.py:57
  8.2 0.1 fusion.2
  8.3 0.0 collective-permute-done
  8.4 1.7 %gather_fusion = bf16[256,256]{1,0:T(8,128)(2,1)S(1)} fusion(bf16[2,128,256]{2,1,0:T(8,128)(2,1)S(1)} %collective-permute-done, s32[256]{0:T(256)S(1)} %fusion.28), kind=kCustom, calls=%fused_computation | custom fusion | bytes 264192 | tf_op jit(solution)/shard_map/vmap()/gather | solution.py:57
  10.0 0.1 broadcast_select_fusion
  10.1 0.2 fusion.1
  10.3 0.4 select_reduce_fusion
  10.7 0.2 fusion.8
  10.9 0.2 fusion.6
  11.1 1.8 %all-gather.3 = f32[2,2,64]{2,1,0:T(2,128)S(1)} all-gather(f32[1,2,64]{2,1,0:T(2,128)S(1)} %bitcast.67), channel_id=3, replica_groups=mesh['user'=16,'seq'=2] {'seq'}, dimensions={0}, use_global_device_ids=true | all-gather | bytes 1536 | tf_op jit(solution)/shard_map/all_gather | solution.py:20
  12.9 1.8 %all-gather.4 = f32[2,2,64]{2,1,0:T(2,128)S(1)} all-gather(f32[1,2,64]{2,1,0:T(2,128)S(1)} %bitcast.72), channel_id=4, replica_groups=mesh['user'=16,'seq'=2] {'seq'}, dimensions={0}, use_global_device_ids=true | all-gather | bytes 1536 | tf_op jit(solution)/shard_map/all_gather | solution.py:20
  14.7 2.0 %all-gather = f32[4,64,256]{2,1,0:T(8,128)S(1)} all-gather(f32[2,64,256]{2,1,0:T(8,128)S(1)} %fusion.8), channel_id=2, replica_groups=mesh['user'=16,'seq'=2] {'seq'}, dimensions={0}, use_global_device_ids=true | all-gather | bytes 393216 | tf_op jit(solution)/shard_map/all_gather | solution.py:20
  16.7 0.1 constant_dynamic-slice_fusion.2
  16.8 0.1 constant_dynamic-slice_fusion
  16.9 0.1 fusion.30
  17.0 41.3 %all-reduce = (f32[256]{0:T(256)S(1)}, f32[256]{0:T(256)S(1)}) all-reduce(f32[256]{0:T(256)S(1)} %get-tuple-element.20, f32[256]{0:T(256)S(1)} %get-tuple-element.19), channel_id=1, replica_groups=mesh['user'=16,'seq'=2] {'user','seq'}, use_global_device_ids=true, to_apply=%region_5.6 | all-reduce | flops 512 | bytes 4096 | tf_op jit(solution)/shard_map/psum | solution.py:81
  58.4 0.7 %copy-done.3 = f32[256]{0:T(256)S(1)} copy-done((f32[256]{0:T(256)S(1)}, f32[256]{0:T(256)}, u32[]{:S(2)}) %copy-start.3) | copy-done | bytes 1048
  59.0 0.6 %add_convert_fusion = bf16[2,32,256]{2,1,0:T(8,128)(2,1)} fusion(f32[2,32,256]{2,1,0:T(8,128)S(1)} %get-tuple-element.23, f32[256]{0:T(256)S(1)} %copy-done.3, f32[256]{0:T(256)S(1)} %copy-done.4, f32[256]{0:T(256)S(1)} %get-tuple-element.40, f32[256]{0:T(256)S(1)} %get-tuple-element.39), kind=kLoop, calls=%fused_computation.15 | loop fusion | flops 81920 | bytes 102400 | tf_op jit(solution)/shard_map/convert_element_type | solution.py:88
  (18 shorter events, 0.1 us)
Async XLA Ops:
  0.0 8.2 %copy-start = (bf16[256,64]{0,1:T(8,128)(2,1)S(1)}, bf16[256,64]{0,1:T(8,128)(2,1)}, u32[]{:S(2)}) copy-start(bf16[256,64]{0,1:T(8,128)(2,1)} %param.11) | copy-start | bytes 98308
  0.0 3.4 %copy-start.2 = (s32[2,1,128]{2,1,0:T(1,128)S(1)}, s32[2,1,128]{2,1,0:T(1,128)}, u32[]{:S(2)}) copy-start(s32[2,1,128]{2,1,0:T(1,128)} %param.9) | copy-start | bytes 3076
  0.0 3.4 %copy-start.5 = (s32[2]{0:T(128)S(1)}, s32[2]{0:T(128)}, u32[]{:S(2)}) copy-start(s32[2]{0:T(128)} %param.10) | copy-start | bytes 28
  1.0 2.6 %copy-start.1 = (bf16[2,32,256]{2,1,0:T(8,128)(2,1)S(1)}, bf16[2,32,256]{2,1,0:T(8,128)(2,1)}, u32[]{:S(2)}) copy-start(bf16[2,32,256]{2,1,0:T(8,128)(2,1)} %param.8) | copy-start | bytes 98308
  1.0 7.4 %collective-permute-start = (bf16[2,128,256]{2,1,0:T(8,128)(2,1)S(1)}, bf16[2,128,256]{2,1,0:T(8,128)(2,1)S(1)}, u32[]{:S(2)}, u32[]{:S(2)}) collective-permute-start(bf16[2,128,256]{2,1,0:T(8,128)(2,1)S(1)} %slice.15), channel_id=1, source_target_pairs={{0,1},{2,3},{4,5},{6,7},{8,9},{10,11},{12,13},{14,15},{16,17},{18,... | collective-permute-start | bytes 393224 | tf_op jit(solution)/shard_map/ppermute | solution.py:16
  16.9 41.5 %copy-start.4 = (f32[256]{0:T(256)S(1)}, f32[256]{0:T(256)}, u32[]{:S(2)}) copy-start(f32[256]{0:T(256)} %param.12) | copy-start | bytes 3076
  58.4 0.7 %copy-start.3 = (f32[256]{0:T(256)S(1)}, f32[256]{0:T(256)}, u32[]{:S(2)}) copy-start(f32[256]{0:T(256)} %param.13) | copy-start | bytes 3076
where the time goes:
time: 60 us; the launch traced here: 59.7 us
  blocking collectives  48.8 us (81%)
  local copies, waits for them, and re-layouts  6.23 us (10%)
  starting transfers between devices  2.41 us (4%)
  other arithmetic  1.14 us (2%)
  matrix products  0.95 us (2%)
    psum x1, blocking collectives, shards(): lax.psum((jnp.sum(attended, axis=(0, 1)), jnp.sum(attended * attended, ax...  41.3 us
    all_gather x3, blocking collectives, joined(): everything = jax.tree.map(lambda part: lax.all_gather(part, axis), shard)  5.58 us
    gather x2, local copies, waits for them, and re-layouts, shards(): take_rows = jax.vmap(lambda row_table, where_at: row_table[where_at])  4.41 us
    ppermute x1, starting transfers between devices, passed_along(): lax.ppermute(value, axis, [(source, source + steps) for source in range(f...  2.41 us
    all_gather x1, blocking collectives, shards(): queries = lax.all_gather(candidates, 'seq', axis=1, tiled=True)  1.85 us
  transfers between devices with their start and end apart: 1, of which 0 were waited for; matrix products, arithmetic and copies ran while one was open for 5% of the time, Pallas kernels for 0%

commit v1 on v0

--- a/solution.py
+++ b/solution.py
@@ -42,6 +42,12 @@
 
 
 def shards(behaviors, candidates, ranks, lengths, hash_planes, norm_gain, norm_bias):
+
+    def extend_series_all(block_in, peer_axis, link_axis):
+        outer = jax.lax.psum(block_in, peer_axis)
+        block_out = jax.lax.psum(outer, link_axis)
+        return block_out
+
     group_rows = behaviors.shape[1]
     feature_width = behaviors.shape[2]
     own_cands = candidates.shape[1]
@@ -78,8 +84,8 @@
     denominator = lax.dynamic_slice_in_dim(merged[1], seq_index * own_cands, own_cands, 1)
     numerator = lax.dynamic_slice_in_dim(merged[2], seq_index * own_cands, own_cands, 1)
     attended = numerator / denominator[..., None]
-    moments = lax.psum(
-        (jnp.sum(attended, axis=(0, 1)), jnp.sum(attended * attended, axis=(0, 1))), ("user", "seq")
+    moments = extend_series_all(
+        (jnp.sum(attended, axis=(0, 1)), jnp.sum(attended * attended, axis=(0, 1))), "seq", "user"
     )
     row_count = attended.shape[0] * own_cands * lax.axis_size("user") * lax.axis_size("seq")
     feature_mean = moments[0] / row_count

time: 60 us -> 64 us (1.067)
  blocking collectives: 48.8 us -> 52.8 us
    psum x1 -> x2, blocking collectives: 41.3 us -> 45.3 us  [the longest x1 42.8 us: extend_series_all(): block_out = jax.lax.psum(outer, link_axis)]
where the time goes in v1:
time: 64 us; the launch traced here: 63.6 us
  blocking collectives  52.8 us (82%)
  local copies, waits for them, and re-layouts  6.24 us (10%)
  starting transfers between devices  2.41 us (4%)
  other arithmetic  1.15 us (2%)
  matrix products  0.95 us (1%)
    psum x1, blocking collectives, extend_series_all(): block_out = jax.lax.psum(outer, link_axis)  42.8 us
    all_gather x3, blocking collectives, joined(): everything = jax.tree.map(lambda part: lax.all_gather(part, axis), shard)  5.58 us
    gather x2, local copies, waits for them, and re-layouts, shards(): take_rows = jax.vmap(lambda row_table, where_at: row_table[where_at])  4.41 us
    psum x1, blocking collectives, extend_series_all(): outer = jax.lax.psum(block_in, peer_axis)  2.47 us
    ppermute x1, starting transfers between devices, passed_along(): lax.ppermute(value, axis, [(source, source + steps) for source in range(f...  2.41 us
    all_gather x1, blocking collectives, shards(): queries = lax.all_gather(candidates, 'seq', axis=1, tiled=True)  1.85 us
  transfers between devices with their start and end apart: 1, of which 0 were waited for; matrix products, arithmetic and copies ran while one was open for 5% of the time, Pallas kernels for 0%

profile of v1, /device:TPU:0, one launch (start us, length us, event | category | flops | bytes accessed | tf_op | source)
XLA Modules:
  0.0 63.6 jit_solution(10260946110632408106)
XLA Ops:
  0.0 0.9 %slice.15 = bf16[2,128,256]{2,1,0:T(8,128)(2,1)S(1)} slice(bf16[2,1024,256]{2,1,0:T(8,128)(2,1)} %param.7), slice={[0:2], [896:1024], [0:256]} | slice | bytes 262144 | tf_op jit(solution)/shard_map/slice | solution.py:56
  1.0 0.0 copy-start.1
  1.0 2.4 %collective-permute-start = (bf16[2,128,256]{2,1,0:T(8,128)(2,1)S(1)}, bf16[2,128,256]{2,1,0:T(8,128)(2,1)S(1)}, u32[]{:S(2)}, u32[]{:S(2)}) collective-permute-start(bf16[2,128,256]{2,1,0:T(8,128)(2,1)S(1)} %slice.15), channel_id=1, source_target_pairs={{0,1},{2,3},{4,5},{6,7},{8,9},{10,11},{12,13},{14,15},{16,17},{18,... | collective-permute-start | bytes 393224 | tf_op jit(solution)/shard_map/ppermute | solution.py:16
  3.4 0.1 compare_and_fusion
  3.5 1.9 %all_gather.21 = bf16[2,64,256]{2,1,0:T(8,128)(2,1)S(1)} all-gather(bf16[2,32,256]{2,1,0:T(8,128)(2,1)S(1)} %copy-done.1), channel_id=1, replica_groups=mesh['user'=16,'seq'=2] {'seq'}, dimensions={1}, use_global_device_ids=true | all-gather | bytes 98304 | tf_op jit(solution)/shard_map/all_gather | solution.py:58
  5.4 2.8 %gather_fusion.1 = bf16[256,256]{1,0:T(8,128)(2,1)S(1)} fusion(bf16[2,1024,256]{2,1,0:T(8,128)(2,1)} %param.7, s32[256]{0:T(256)S(1)} %fusion.27), kind=kCustom, calls=%fused_computation.1 | custom fusion | bytes 264192 | tf_op jit(solution)/shard_map/vmap()/gather | solution.py:63
  8.2 0.1 fusion.2
  8.3 0.0 collective-permute-done
  8.4 1.7 %gather_fusion = bf16[256,256]{1,0:T(8,128)(2,1)S(1)} fusion(bf16[2,128,256]{2,1,0:T(8,128)(2,1)S(1)} %collective-permute-done, s32[256]{0:T(256)S(1)} %fusion.28), kind=kCustom, calls=%fused_computation | custom fusion | bytes 264192 | tf_op jit(solution)/shard_map/vmap()/gather | solution.py:63
  10.0 0.1 broadcast_select_fusion
  10.1 0.2 fusion.1
  10.3 0.4 select_reduce_fusion
  10.7 0.2 fusion.8
  10.9 0.2 fusion.6
  11.1 1.8 %all-gather.3 = f32[2,2,64]{2,1,0:T(2,128)S(1)} all-gather(f32[1,2,64]{2,1,0:T(2,128)S(1)} %bitcast.67), channel_id=3, replica_groups=mesh['user'=16,'seq'=2] {'seq'}, dimensions={0}, use_global_device_ids=true | all-gather | bytes 1536 | tf_op jit(solution)/shard_map/all_gather | solution.py:20
  12.9 1.8 %all-gather.4 = f32[2,2,64]{2,1,0:T(2,128)S(1)} all-gather(f32[1,2,64]{2,1,0:T(2,128)S(1)} %bitcast.72), channel_id=4, replica_groups=mesh['user'=16,'seq'=2] {'seq'}, dimensions={0}, use_global_device_ids=true | all-gather | bytes 1536 | tf_op jit(solution)/shard_map/all_gather | solution.py:20
  14.7 2.0 %all-gather = f32[4,64,256]{2,1,0:T(8,128)S(1)} all-gather(f32[2,64,256]{2,1,0:T(8,128)S(1)} %fusion.8), channel_id=2, replica_groups=mesh['user'=16,'seq'=2] {'seq'}, dimensions={0}, use_global_device_ids=true | all-gather | bytes 393216 | tf_op jit(solution)/shard_map/all_gather | solution.py:20
  16.7 0.1 constant_dynamic-slice_fusion.2
  16.8 0.1 constant_dynamic-slice_fusion
  16.9 0.1 fusion.30
  17.0 2.5 %all-reduce.1 = (f32[256]{0:T(256)S(1)}, f32[256]{0:T(256)S(1)}) all-reduce(f32[256]{0:T(256)S(1)} %get-tuple-element.20, f32[256]{0:T(256)S(1)} %get-tuple-element.19), channel_id=1, replica_groups=mesh['user'=16,'seq'=2] {'seq'}, use_global_device_ids=true, to_apply=%region_6.7 | all-reduce | flops 512 | bytes 4096 | tf_op jit(solution)/shard_map/psum | solution.py:47
  19.5 42.8 %all-reduce = (f32[256]{0:T(256)S(1)}, f32[256]{0:T(256)S(1)}) all-reduce(f32[256]{0:T(256)S(1)} %get-tuple-element.23, f32[256]{0:T(256)S(1)} %get-tuple-element.32), channel_id=1, replica_groups=mesh['user'=16,'seq'=2] {'user'}, use_global_device_ids=true, to_apply=%region_7.8 | all-reduce | flops 512 | bytes 4096 | tf_op jit(solution)/shard_map/psum | solution.py:48
  62.3 0.7 %copy-done.3 = f32[256]{0:T(256)S(1)} copy-done((f32[256]{0:T(256)S(1)}, f32[256]{0:T(256)}, u32[]{:S(2)}) %copy-start.3) | copy-done | bytes 1048
  63.0 0.6 add_convert_fusion
  (19 shorter events, 0.1 us)
Async XLA Ops:
  0.0 8.2 %copy-start = (bf16[256,64]{0,1:T(8,128)(2,1)S(1)}, bf16[256,64]{0,1:T(8,128)(2,1)}, u32[]{:S(2)}) copy-start(bf16[256,64]{0,1:T(8,128)(2,1)} %param.11) | copy-start | bytes 98308
  0.0 3.4 %copy-start.2 = (s32[2,1,128]{2,1,0:T(1,128)S(1)}, s32[2,1,128]{2,1,0:T(1,128)}, u32[]{:S(2)}) copy-start(s32[2,1,128]{2,1,0:T(1,128)} %param.9) | copy-start | bytes 3076
  0.0 3.4 %copy-start.5 = (s32[2]{0:T(128)S(1)}, s32[2]{0:T(128)}, u32[]{:S(2)}) copy-start(s32[2]{0:T(128)} %param.10) | copy-start | bytes 28
  1.0 2.6 %copy-start.1 = (bf16[2,32,256]{2,1,0:T(8,128)(2,1)S(1)}, bf16[2,32,256]{2,1,0:T(8,128)(2,1)}, u32[]{:S(2)}) copy-start(bf16[2,32,256]{2,1,0:T(8,128)(2,1)} %param.8) | copy-start | bytes 98308
  1.0 7.4 %collective-permute-start = (bf16[2,128,256]{2,1,0:T(8,128)(2,1)S(1)}, bf16[2,128,256]{2,1,0:T(8,128)(2,1)S(1)}, u32[]{:S(2)}, u32[]{:S(2)}) collective-permute-start(bf16[2,128,256]{2,1,0:T(8,128)(2,1)S(1)} %slice.15), channel_id=1, source_target_pairs={{0,1},{2,3},{4,5},{6,7},{8,9},{10,11},{12,13},{14,15},{16,17},{18,... | collective-permute-start | bytes 393224 | tf_op jit(solution)/shard_map/ppermute | solution.py:16
  16.9 45.4 %copy-start.4 = (f32[256]{0:T(256)S(1)}, f32[256]{0:T(256)}, u32[]{:S(2)}) copy-start(f32[256]{0:T(256)} %param.12) | copy-start | bytes 3076
  62.3 0.7 %copy-start.3 = (f32[256]{0:T(256)S(1)}, f32[256]{0:T(256)}, u32[]{:S(2)}) copy-start(f32[256]{0:T(256)} %param.13) | copy-start | bytes 3076
